TPU v7x, 512 devices: a whole 4x8x8 slice. The times are simulated.
512 devices in a mesh: leaf: 128 (over z, y, core), rhs: 4 (over x).
Axes of the slice: x: 4, y: 8, z: 8, core: 2. Of those that a mesh axis runs over, the one named last changes fastest.
Arguments:
- right_sides: bfloat16 [512, 131072], P('rhs', 'leaf'), may hold values from -6 to 6
- block_order: int32 [1024], replicated, may hold values from 0 to 1023, each once
- leaf_basis: bfloat16 [128, 1024, 256], P('leaf'), may hold values from -0.1875 to 0.1875
- leaf_inner: bfloat16 [128, 256, 256], P('leaf'), may hold values from -0.375 to 0.375
- leaf_inverse: bfloat16 [128, 768, 768], P('leaf', 'rhs'), may hold values from -0.21875 to 0.21875
- leaf_coupling: bfloat16 [128, 768, 256], P('leaf'), may hold values from -0.21875 to 0.21875
- merge_one: bfloat16 [32768, 512], P('leaf'), may hold values from -0.25 to 0.25
- merge_two: bfloat16 [16384, 512], P('leaf'), may hold values from -0.25 to 0.25
- merge_three: bfloat16 [8192, 512], P('leaf'), may hold values from -0.25 to 0.25
Outputs:
- leaf_part: bfloat16 [512, 98304], P('rhs', 'leaf')
- level_one: float32 [512, 16384], P('rhs', 'leaf')
- level_two: float32 [512, 8192], P('rhs', 'leaf')
- level_three: float32 [512, 4096], P('rhs', 'leaf')
- top_skeleton: float32 [512, 4096], P('rhs', 'leaf')
Inputs may be any that keep to these rules, and one draw needn't show every extreme that they name: block_order is a permutation: every block of the 1024 appears exactly once.
All inputs are finite; a program needn't handle non-finite values.
Results may differ from a plain program's by a relative error of at most 0.007.
Values may be sent and summed in bfloat16 or wider, within the bound.
A program may use at most 64 MiB of HBM per device.

v0:
```python
import jax
import jax.numpy as jnp
from jax import lax
from jax.sharding import PartitionSpec as P

BLOCK = 128


def swapped(block, axis, bit):
    count = lax.axis_size(axis)
    route = []
    for low in range(count):
        high = low | 1 << bit
        if high != low and high < count:
            route += [(low, high), (high, low)]
    return lax.ppermute(block, axis, route)


def shards(
    right_sides,
    block_order,
    leaf_basis,
    leaf_inner,
    leaf_inverse,
    leaf_coupling,
    merge_one,
    merge_two,
    merge_three,
):
    leaf_count = lax.axis_size("leaf")
    columns, row_count = right_sides.shape
    per_group = columns // leaf_count
    group_size = per_group * row_count
    tile_width = 128
    outgoing = right_sides.reshape(leaf_count, group_size // tile_width, tile_width)
    arrived = lax.all_to_all(outgoing, "leaf", split_axis=0, concat_axis=1, tiled=True)
    full_rows = jnp.transpose(arrived.reshape(leaf_count, per_group, row_count), (1, 0, 2))
    blocks = full_rows.reshape(per_group, -1, BLOCK)
    reordered = jnp.take(blocks, block_order, axis=1).reshape(per_group, leaf_count, row_count)
    returning = jnp.transpose(reordered, (1, 0, 2)).reshape(
        leaf_count, group_size // tile_width, tile_width
    )
    placed = lax.all_to_all(returning, "leaf", split_axis=0, concat_axis=1, tiled=True).reshape(
        columns, row_count
    )
    basis_matrix = leaf_basis[0]
    projected = jnp.dot(placed, basis_matrix, preferred_element_type=jnp.float32).astype(
        jnp.bfloat16
    )
    middle = jnp.dot(projected, leaf_inner[0], preferred_element_type=jnp.float32).astype(
        jnp.bfloat16
    )
    correction = lax.dot_general(
        middle, basis_matrix, (((1,), (1,)), ((), ())), preferred_element_type=jnp.float32
    )
    reflected = (placed.astype(jnp.float32) - correction).astype(jnp.bfloat16)
    split_at = row_count - basis_matrix.shape[1]
    leading = reflected[:, :split_at]
    trailing = reflected[:, split_at:]
    eliminated = jnp.dot(
        leading,
        lax.all_gather(leaf_inverse, "rhs", axis=1, tiled=True)[0],
        preferred_element_type=jnp.float32,
    ).astype(jnp.bfloat16)
    coupled = jnp.dot(eliminated, leaf_coupling[0], preferred_element_type=jnp.float32)
    current = (trailing.astype(jnp.float32) - coupled).astype(jnp.bfloat16)
    position = lax.axis_index("leaf")
    outputs = []
    top_part = None
    for level_index, merge_table in enumerate((merge_one, merge_two, merge_three), start=1):
        contribution = jnp.dot(current, merge_table, preferred_element_type=jnp.float32)
        group_count = 2**level_index
        piece_width = contribution.shape[1] // group_count
        shares = contribution.reshape(columns, group_count, piece_width)
        for bit_index in reversed(range(level_index)):
            half_count = shares.shape[1] // 2
            lower_half = shares[:, :half_count]
            upper_half = shares[:, half_count:]
            upper_side = position >> bit_index & 1 == 1
            retained = jnp.where(upper_side, upper_half, lower_half)
            outgoing_half = jnp.where(upper_side, lower_half, upper_half)
            shares = retained + swapped(outgoing_half, "leaf", bit_index)
        own_group = shares.reshape(columns, piece_width)
        outputs.append(own_group[:, : piece_width // 2])
        top_part = own_group[:, piece_width // 2 :]
        current = top_part.astype(jnp.bfloat16)
    return (eliminated, outputs[0], outputs[1], outputs[2], top_part)


def solution(mesh):
    placed = (
        P("rhs", "leaf"),
        P(),
        P("leaf", None, None),
        P("leaf", None, None),
        P("leaf", "rhs", None),
        P("leaf", None, None),
        P("leaf", None),
        P("leaf", None),
        P("leaf", None),
    )
    return jax.shard_map(
        shards,
        mesh=mesh,
        in_specs=placed,
        out_specs=(
            P("rhs", "leaf"),
            P("rhs", "leaf"),
            P("rhs", "leaf"),
            P("rhs", "leaf"),
            P("rhs", "leaf"),
        ),
        check_vma=False,
    )
```

profile of v0, /device:TPU:1, one launch (start us, length us, event | category | flops | bytes accessed | tf_op | source)
XLA Modules:
  0.0 113.8 jit_solution(4299900038317660262)
XLA Ops:
  7.2 1.8 %copy.29 = bf16[16,8,8,128]{3,2,1,0:T(8,128)(2,1)} copy(bf16[16,8,8,128]{3,1,2,0:T(8,128)(2,1)} %bitcast.49) | data formatting | bytes 524288
  9.0 18.4 %all-to-all-start = ((bf16[128,8,128]{2,1,0:T(8,128)(2,1)}), bf16[128,8,128]{2,1,0:T(8,128)(2,1)S(1)}, u32[]{:S(2)}, u32[]{:S(2)}) async-start(bf16[128,8,128]{2,1,0:T(8,128)(2,1)} %bitcast.12), calls=%async_computation | async-start | bytes 524288 | tf_op jit(solution)/shard_map/all_to_all | solution.py:36
  27.4 0.7 all-gather.2.cloned.1.call-update
  28.3 14.4 %all-to-all-done = bf16[128,8,128]{2,1,0:T(8,128)(2,1)S(1)} async-done(((bf16[128,8,128]{2,1,0:T(8,128)(2,1)}), bf16[128,8,128]{2,1,0:T(8,128)(2,1)S(1)}, u32[]{:S(2)}, u32[]{:S(2)}) %all-to-all-start) | async-done | bytes 262176 | tf_op jit(solution)/shard_map/all_to_all | solution.py:36
  42.6 3.2 %gather_fusion = bf16[1024,128]{1,0:T(8,128)(2,1)S(1)} fusion(bf16[1024,128]{1,0:T(8,128)(2,1)S(1)} %bitcast.42, s32[1024]{0:T(1024)S(1)} %fusion.23), kind=kCustom, calls=%fused_computation | custom fusion | bytes 528384 | tf_op jit(solution)/shard_map/jit(_take)/gather | solution.py:39
  45.8 0.9 bitcast_select_fusion
  46.7 5.5 %all-to-all-start.1 = ((bf16[128,8,128]{2,1,0:T(8,128)(2,1)}), bf16[128,8,128]{2,1,0:T(8,128)(2,1)S(1)}, u32[]{:S(2)}, u32[]{:S(2)}) async-start(bf16[128,8,128]{2,1,0:T(8,128)(2,1)} %bitcast_select_fusion), calls=%async_computation.1 | async-start | bytes 524288 | tf_op jit(solution)/shard_map/all_to_all | solution.py:43
  52.3 15.3 %all-to-all-done.1 = bf16[128,8,128]{2,1,0:T(8,128)(2,1)S(1)} async-done(((bf16[128,8,128]{2,1,0:T(8,128)(2,1)}), bf16[128,8,128]{2,1,0:T(8,128)(2,1)S(1)}, u32[]{:S(2)}, u32[]{:S(2)}) %all-to-all-start.1) | async-done | bytes 262176 | tf_op jit(solution)/shard_map/all_to_all | solution.py:43
  68.4 1.6 %fusion.3 = bf16[128,768]{1,0:T(8,128)(2,1)S(1)} fusion(bf16[1,768,768]{2,1,0:T(8,128)(2,1)} %all-gather.2.cloned.1.call-done, bf16[128,1024]{1,0:T(8,128)(2,1)S(1)} %fusion), kind=kOutput, calls=%fused_computation.5 | convolution fusion | flops 151093248 | bytes 1572864 | tf_op jit(solution)/shard_map/dot_general | solution.py:60
  70.0 0.4 fusion.7
  70.9 2.3 %collective-permute-start = (f32[128,1,256]{2,0,1:T(8,128)S(1)}, f32[128,1,256]{2,0,1:T(8,128)S(1)}, u32[]{:S(2)}, u32[]{:S(2)}) collective-permute-start(f32[128,1,256]{2,0,1:T(8,128)S(1)} %copy_select_fusion), channel_id=1, source_target_pairs={{0,4},{4,0},{8,12},{12,8},{16,20},{20,16},{24,28},{28,24},{32,36},... | collective-permute-start | bytes 393224 | tf_op jit(solution)/shard_map/ppermute | solution.py:16
  73.2 0.9 collective-permute-done
  74.4 2.7 %collective-permute-start.1 = (f32[128,2,128]{0,2,1:T(8,128)S(1)}, f32[128,2,128]{0,2,1:T(8,128)S(1)}, u32[]{:S(2)}, u32[]{:S(2)}) collective-permute-start(f32[128,2,128]{0,2,1:T(8,128)S(1)} %slice_select_fusion.1), channel_id=1, source_target_pairs={{0,8},{8,0},{4,12},{12,4},{16,24},{24,16},{20,28},{28,20},{32,40},... | collective-permute-start | bytes 393224 | tf_op jit(solution)/shard_map/ppermute | solution.py:16
  77.2 3.9 %collective-permute-done.1 = f32[128,2,128]{0,2,1:T(8,128)S(1)} collective-permute-done((f32[128,2,128]{0,2,1:T(8,128)S(1)}, f32[128,2,128]{0,2,1:T(8,128)S(1)}, u32[]{:S(2)}, u32[]{:S(2)}) %collective-permute-start.1) | collective-permute-done | bytes 131104 | tf_op jit(solution)/shard_map/ppermute | solution.py:16
  81.1 3.1 %collective-permute-start.2 = (f32[128,1,128]{0,2,1:T(8,128)S(1)}, f32[128,1,128]{0,2,1:T(8,128)S(1)}, u32[]{:S(2)}, u32[]{:S(2)}) collective-permute-start(f32[128,1,128]{0,2,1:T(8,128)S(1)} %slice_select_fusion.3), channel_id=1, source_target_pairs={{0,4},{4,0},{8,12},{12,8},{16,20},{20,16},{24,28},{28,24},{32,36},... | collective-permute-start | bytes 196616 | tf_op jit(solution)/shard_map/ppermute | solution.py:16
  84.2 0.9 collective-permute-done.2
  85.4 2.8 %collective-permute-start.3 = (f32[128,4,64]{0,2,1:T(8,128)S(1)}, f32[128,4,64]{0,2,1:T(8,128)S(1)}, u32[]{:S(2)}, u32[]{:S(2)}) collective-permute-start(f32[128,4,64]{0,2,1:T(8,128)S(1)} %slice_select_fusion), channel_id=1, source_target_pairs={{0,16},{16,0},{4,20},{20,4},{8,24},{24,8},{12,28},{28,12},{32,48},... | collective-permute-start | bytes 393224 | tf_op jit(solution)/shard_map/ppermute | solution.py:16
  88.2 7.6 %collective-permute-done.3 = f32[128,4,64]{0,2,1:T(8,128)S(1)} collective-permute-done((f32[128,4,64]{0,2,1:T(8,128)S(1)}, f32[128,4,64]{0,2,1:T(8,128)S(1)}, u32[]{:S(2)}, u32[]{:S(2)}) %collective-permute-start.3) | collective-permute-done | bytes 131104 | tf_op jit(solution)/shard_map/ppermute | solution.py:16
  95.9 1.9 %collective-permute-start.4 = (f32[128,2,64]{0,2,1:T(8,128)S(1)}, f32[128,2,64]{0,2,1:T(8,128)S(1)}, u32[]{:S(2)}, u32[]{:S(2)}) collective-permute-start(f32[128,2,64]{0,2,1:T(8,128)S(1)} %slice_select_fusion.2), channel_id=1, source_target_pairs={{0,8},{8,0},{4,12},{12,4},{16,24},{24,16},{20,28},{28,20},{32,40},... | collective-permute-start | bytes 196616 | tf_op jit(solution)/shard_map/ppermute | solution.py:16
  97.8 3.1 %collective-permute-done.4 = f32[128,2,64]{0,2,1:T(8,128)S(1)} collective-permute-done((f32[128,2,64]{0,2,1:T(8,128)S(1)}, f32[128,2,64]{0,2,1:T(8,128)S(1)}, u32[]{:S(2)}, u32[]{:S(2)}) %collective-permute-start.4) | collective-permute-done | bytes 65568 | tf_op jit(solution)/shard_map/ppermute | solution.py:16
  100.9 4.1 %collective-permute-start.5 = (f32[128,1,64]{0,2,1:T(8,128)S(1)}, f32[128,1,64]{0,2,1:T(8,128)S(1)}, u32[]{:S(2)}, u32[]{:S(2)}) collective-permute-start(f32[128,1,64]{0,2,1:T(8,128)S(1)} %slice_select_fusion.4), channel_id=1, source_target_pairs={{0,4},{4,0},{8,12},{12,8},{16,20},{20,16},{24,28},{28,24},{32,36},... | collective-permute-start | bytes 98312 | tf_op jit(solution)/shard_map/ppermute | solution.py:16
  105.0 0.6 slice.88
  105.7 0.6 slice.94
  106.3 0.6 fusion.25
  (40 shorter events, 1.9 us)
Async XLA Ops:
  7.2 60.5 %copy-start = (bf16[1,1024,256]{2,1,0:T(8,128)(2,1)S(1)}, bf16[1,1024,256]{2,1,0:T(8,128)(2,1)}, u32[]{:S(2)}) copy-start(bf16[1,1024,256]{2,1,0:T(8,128)(2,1)} %param.11) | copy-start | bytes 1572868
  7.2 20.9 %copy-start.7 = (s32[1024]{0:T(1024)S(1)}, s32[1024]{0:T(1024)}, u32[]{:S(2)}) copy-start(s32[1024]{0:T(1024)} %param.10) | copy-start | bytes 12292
  9.0 33.6 %all-to-all-start = ((bf16[128,8,128]{2,1,0:T(8,128)(2,1)}), bf16[128,8,128]{2,1,0:T(8,128)(2,1)S(1)}, u32[]{:S(2)}, u32[]{:S(2)}) async-start(bf16[128,8,128]{2,1,0:T(8,128)(2,1)} %bitcast.12), calls=%async_computation | async-start | bytes 524288 | tf_op jit(solution)/shard_map/all_to_all | solution.py:36
  27.4 41.0 %all-gather.2.cloned.1.call-start = ((), (), s32[]{:S(2)}) async-start(), calls=%async_computation.2 | async-start | bytes 1474560 | tf_op jit(solution)/shard_map/all_gather | solution.py:62
  42.6 25.0 %copy-start.4 = (bf16[1,256,256]{2,1,0:T(8,128)(2,1)S(1)}, bf16[1,256,256]{2,1,0:T(8,128)(2,1)}, u32[]{:S(2)}) copy-start(bf16[1,256,256]{2,1,0:T(8,128)(2,1)} %param.12) | copy-start | bytes 393220
  46.7 20.9 %all-to-all-start.1 = ((bf16[128,8,128]{2,1,0:T(8,128)(2,1)}), bf16[128,8,128]{2,1,0:T(8,128)(2,1)S(1)}, u32[]{:S(2)}, u32[]{:S(2)}) async-start(bf16[128,8,128]{2,1,0:T(8,128)(2,1)} %bitcast_select_fusion), calls=%async_computation.1 | async-start | bytes 524288 | tf_op jit(solution)/shard_map/all_to_all | solution.py:43
  68.0 2.0 %copy-start.2 = (bf16[1,768,256]{2,1,0:T(8,128)(2,1)S(1)}, bf16[1,768,256]{2,1,0:T(8,128)(2,1)}, u32[]{:S(2)}) copy-start(bf16[1,768,256]{2,1,0:T(8,128)(2,1)} %param.14) | copy-start | bytes 1179652
  68.0 2.0 %copy-start.3 = (bf16[256,512]{1,0:T(8,128)(2,1)S(1)}, bf16[256,512]{1,0:T(8,128)(2,1)}, u32[]{:S(2)}) copy-start(bf16[256,512]{1,0:T(8,128)(2,1)} %param.15) | copy-start | bytes 786436
  70.0 0.9 copy-start.1
  70.4 3.7 %copy-start.5 = (bf16[128,512]{1,0:T(8,128)(2,1)S(1)}, bf16[128,512]{1,0:T(8,128)(2,1)}, u32[]{:S(2)}) copy-start(bf16[128,512]{1,0:T(8,128)(2,1)} %param.16) | copy-start | bytes 393220
  70.9 3.3 %collective-permute-start = (f32[128,1,256]{2,0,1:T(8,128)S(1)}, f32[128,1,256]{2,0,1:T(8,128)S(1)}, u32[]{:S(2)}, u32[]{:S(2)}) collective-permute-start(f32[128,1,256]{2,0,1:T(8,128)S(1)} %copy_select_fusion), channel_id=1, source_target_pairs={{0,4},{4,0},{8,12},{12,8},{16,20},{20,16},{24,28},{28,24},{32,36},... | collective-permute-start | bytes 393224 | tf_op jit(solution)/shard_map/ppermute | solution.py:16
  73.2 11.9 %copy-start.6 = (bf16[64,512]{1,0:T(8,128)(2,1)S(1)}, bf16[64,512]{1,0:T(8,128)(2,1)}, u32[]{:S(2)}) copy-start(bf16[64,512]{1,0:T(8,128)(2,1)} %param.17) | copy-start | bytes 196612
  74.4 6.6 %collective-permute-start.1 = (f32[128,2,128]{0,2,1:T(8,128)S(1)}, f32[128,2,128]{0,2,1:T(8,128)S(1)}, u32[]{:S(2)}, u32[]{:S(2)}) collective-permute-start(f32[128,2,128]{0,2,1:T(8,128)S(1)} %slice_select_fusion.1), channel_id=1, source_target_pairs={{0,8},{8,0},{4,12},{12,4},{16,24},{24,16},{20,28},{28,20},{32,40},... | collective-permute-start | bytes 393224 | tf_op jit(solution)/shard_map/ppermute | solution.py:16
  81.1 4.0 %collective-permute-start.2 = (f32[128,1,128]{0,2,1:T(8,128)S(1)}, f32[128,1,128]{0,2,1:T(8,128)S(1)}, u32[]{:S(2)}, u32[]{:S(2)}) collective-permute-start(f32[128,1,128]{0,2,1:T(8,128)S(1)} %slice_select_fusion.3), channel_id=1, source_target_pairs={{0,4},{4,0},{8,12},{12,8},{16,20},{20,16},{24,28},{28,24},{32,36},... | collective-permute-start | bytes 196616 | tf_op jit(solution)/shard_map/ppermute | solution.py:16
  85.4 10.5 %collective-permute-start.3 = (f32[128,4,64]{0,2,1:T(8,128)S(1)}, f32[128,4,64]{0,2,1:T(8,128)S(1)}, u32[]{:S(2)}, u32[]{:S(2)}) collective-permute-start(f32[128,4,64]{0,2,1:T(8,128)S(1)} %slice_select_fusion), channel_id=1, source_target_pairs={{0,16},{16,0},{4,20},{20,4},{8,24},{24,8},{12,28},{28,12},{32,48},... | collective-permute-start | bytes 393224 | tf_op jit(solution)/shard_map/ppermute | solution.py:16
  95.9 5.0 %collective-permute-start.4 = (f32[128,2,64]{0,2,1:T(8,128)S(1)}, f32[128,2,64]{0,2,1:T(8,128)S(1)}, u32[]{:S(2)}, u32[]{:S(2)}) collective-permute-start(f32[128,2,64]{0,2,1:T(8,128)S(1)} %slice_select_fusion.2), channel_id=1, source_target_pairs={{0,8},{8,0},{4,12},{12,4},{16,24},{24,16},{20,28},{28,20},{32,40},... | collective-permute-start | bytes 196616 | tf_op jit(solution)/shard_map/ppermute | solution.py:16
  100.9 5.4 %collective-permute-start.5 = (f32[128,1,64]{0,2,1:T(8,128)S(1)}, f32[128,1,64]{0,2,1:T(8,128)S(1)}, u32[]{:S(2)}, u32[]{:S(2)}) collective-permute-start(f32[128,1,64]{0,2,1:T(8,128)S(1)} %slice_select_fusion.4), channel_id=1, source_target_pairs={{0,4},{4,0},{8,12},{12,8},{16,20},{20,16},{24,28},{28,24},{32,36},... | collective-permute-start | bytes 98312 | tf_op jit(solution)/shard_map/ppermute | solution.py:16
Sparse Core Ops, SparseCore 0:
  30.3 28.4 all-gather.1
where the time goes:
time: 114 us
  waiting for transfers between devices  46.8 us (41%)
  starting transfers between devices  41 us (36%)
  between operations  14.4 us (13%)
  local copies, waits for them, and re-layouts  7.36 us (6%)
  matrix products  3.14 us (3%)
    all_to_all x1, starting transfers between devices, shards(): lax.all_to_all(outgoing, 'leaf', split_axis=0, concat_axis=1, tiled=True)  18.4 us
    ppermute x6, starting transfers between devices, swapped(): return lax.ppermute(block, axis, route)  17 us
    ppermute x6, waiting for transfers between devices, swapped(): return lax.ppermute(block, axis, route)  16.4 us
    all_to_all x1, waiting for transfers between devices, shards(): lax.all_to_all(returning, 'leaf', split_axis=0, concat_axis=1, tiled=True)  15.3 us
    all_to_all x1, waiting for transfers between devices, shards(): lax.all_to_all(outgoing, 'leaf', split_axis=0, concat_axis=1, tiled=True)  14.4 us
    all_to_all x1, starting transfers between devices, shards(): lax.all_to_all(returning, 'leaf', split_axis=0, concat_axis=1, tiled=True)  5.54 us
    gather x1, local copies, waits for them, and re-layouts, shards(): jnp.take(blocks, block_order, axis=1)  3.2 us
  transfers between devices with their start and end apart: 9, of which 7 were waited for; matrix products, arithmetic and copies ran while one was open for 5% of the time, Pallas kernels for 0%

commit v1 on v0

v1 whole, which is shorter than its diff:
```python
import jax
import jax.numpy as jnp
from jax import lax
from jax.experimental import pallas as pl
from jax.experimental.pallas import tpu as pltpu
from jax.sharding import PartitionSpec as P

BF = jnp.bfloat16
F32 = jnp.float32
CHIPS = 64
GROUP = 8
PLANES = 4


def dot(a, b):
    return jnp.dot(a, b, preferred_element_type=F32)


def kernel(
    order,
    rows_in,
    basis_in,
    inner_in,
    inverse_in,
    coupling_in,
    one_in,
    two_in,
    three_in,
    leaf_out,
    first_out,
    second_out,
    third_out,
    top_out,
    rows,
    pool,
    picked,
    placed,
    flat,
    basis,
    inner,
    inverse,
    coupling,
    one,
    two,
    three,
    w_one,
    w_two,
    w_three,
    s_one,
    s_two,
    s_three,
    o_leaf,
    o_first,
    o_second,
    o_third,
    o_top,
    load_sem,
    own_sem,
    out_sem,
    spread_sem,
    twin_sem,
    gather_sem,
    inv_sem,
    w_sem,
    s_sem,
):
    me = lax.axis_index("leaf")
    plane = lax.axis_index("rhs")
    chip = me // 2
    core = me % 2
    in_group = me % GROUP
    group = me - in_group
    in_quad = me % 4
    quad = me - in_quad
    twin = me + 1 - 2 * core

    loads = [
        (rows_in, rows),
        (inverse_in, inverse.at[pl.ds(pl.multiple_of(plane * 192, 64), 192)]),
        (one_in, one),
        (two_in, two),
        (three_in, three),
        (basis_in, basis),
        (inner_in, inner),
        (coupling_in, coupling),
    ]
    loads = [pltpu.make_async_copy(a, b, load_sem.at[i]) for i, (a, b) in enumerate(loads)]
    for load in loads:
        load.start()

    def remote(src, dst, send, recv, target, axis="leaf"):
        return pltpu.make_async_remote_copy(
            src_ref=src,
            dst_ref=dst,
            send_sem=send,
            recv_sem=recv,
            device_id={axis: target},
            device_id_type=pl.DeviceIdType.MESH,
        )

    barrier = pltpu.get_barrier_semaphore()

    def greet(target, axis="leaf"):
        pl.semaphore_signal(
            barrier, inc=1, device_id={axis: target}, device_id_type=pl.DeviceIdType.MESH
        )

    def greet_chip(k, _):
        greet(lax.rem(chip + k, CHIPS) * 2 + core)
        return 0

    lax.fori_loop(1, CHIPS, greet_chip, 0)
    for i in range(GROUP // 2):
        greet(group + 2 * i + 1 - core)
    for d in range(1, PLANES):
        greet(lax.rem(plane + d, PLANES), "rhs")
    pl.semaphore_wait(barrier, CHIPS - 1 + GROUP // 2 + PLANES - 1)

    loads[0].wait()
    mine = pl.ds(pl.multiple_of((core * CHIPS + chip) * 8, 8), 8)

    def spread(k, _):
        other = lax.rem(chip + k, CHIPS)
        remote(
            rows.at[other // 4, :, other % 4],
            pool.at[mine],
            spread_sem.at[0],
            spread_sem.at[1],
            other * 2 + core,
        ).start()
        return 0

    lax.fori_loop(1, CHIPS, spread, 0)
    own = pltpu.make_async_copy(rows.at[chip // 4, :, chip % 4], pool.at[mine], own_sem.at[0])
    own.start()

    pieces = []
    for load in loads[1:5]:
        load.wait()
    for d in range(1, PLANES):
        share = inverse.at[pl.ds(pl.multiple_of(plane * 192, 64), 192)]
        c = remote(
            share, share, inv_sem.at[0, d], inv_sem.at[1, d], lax.rem(plane + d, PLANES), "rhs"
        )
        c.start()
        pieces.append(c)
    c = remote(
        one.at[:, pl.ds(pl.multiple_of((1 - core) * 256, 256), 256)],
        w_one.at[core],
        w_sem.at[0, 0],
        w_sem.at[1, 0],
        twin,
    )
    c.start()
    pieces.append(c)
    local = [
        pltpu.make_async_copy(
            one.at[:, pl.ds(pl.multiple_of(core * 256, 256), 256)], w_one.at[core], own_sem.at[1]
        ),
        pltpu.make_async_copy(
            two.at[:, pl.ds(pl.multiple_of(in_quad * 128, 128), 128)],
            w_two.at[in_quad],
            own_sem.at[2],
        ),
        pltpu.make_async_copy(
            three.at[:, pl.ds(pl.multiple_of(in_group // 2 * 128, 128), 128)],
            w_three.at[in_group],
            own_sem.at[3],
        ),
    ]
    for c in local:
        c.start()
    for d in range(1, 4):
        other = lax.rem(in_quad + d, 4)
        c = remote(
            two.at[:, pl.ds(pl.multiple_of(other * 128, 128), 128)],
            w_two.at[in_quad],
            w_sem.at[0, d],
            w_sem.at[1, d],
            quad + other,
        )
        c.start()
        pieces.append(c)
    for d in range(1, GROUP):
        other = lax.rem(in_group + d, GROUP)
        c = remote(
            three.at[:, pl.ds(pl.multiple_of(other // 2 * 128, 128), 128)],
            w_three.at[in_group],
            w_sem.at[0, 3 + d],
            w_sem.at[1, 3 + d],
            group + other,
        )
        c.start()
        pieces.append(c)

    own.wait()
    part = pool.at[pl.ds(0, (CHIPS - 1) * 8)]
    pltpu.make_async_copy(part, part, spread_sem.at[1]).wait()
    half = pool.at[pl.ds(pl.multiple_of(core * CHIPS * 8, 8), CHIPS * 8)]
    handed = remote(half, half, twin_sem.at[0], twin_sem.at[1], twin)
    handed.start()
    handed.wait_recv()

    def send(other):
        remote(
            picked.at[other],
            placed.at[:, chip],
            gather_sem.at[0],
            gather_sem.at[1],
            other * 2 + core,
        ).start()

    def gather(k, _):
        other = lax.rem(chip + k, CHIPS)
        first = (other * 2 + core) * 8
        for j in range(8):
            picked[other, j] = pool[order[first + j]]

        @pl.when(k > 1)
        def _():
            send(lax.rem(chip + k - 1, CHIPS))

        return 0

    lax.fori_loop(1, CHIPS + 1, gather, 0)
    own = pltpu.make_async_copy(picked.at[chip], placed.at[:, chip], own_sem.at[0])
    own.start()
    for load in loads[5:]:
        load.wait()
    own.wait()
    part = picked.at[pl.ds(0, CHIPS - 1)]
    pltpu.make_async_copy(part, part, gather_sem.at[1]).wait()

    for j in range(8):
        flat[:, j * 128 : (j + 1) * 128] = placed[j].reshape(128, 128)
    projected = dot(flat[...], basis[...]).astype(BF)
    middle = dot(projected, inner[...]).astype(BF)
    correction = lax.dot_general(
        middle, basis[...], (((1,), (1,)), ((), ())), preferred_element_type=F32
    )
    reflected = (flat[...].astype(F32) - correction).astype(BF)
    for c in pieces[:3]:
        c.wait_recv()
    eliminated = dot(reflected[:, :768], inverse[...]).astype(BF)
    o_leaf[...] = eliminated
    outs = [pltpu.make_async_copy(o_leaf, leaf_out, out_sem.at[0])]
    outs[0].start()
    coupled = dot(eliminated, coupling[...])
    s_one[core] = (reflected[:, 768:].astype(F32) - coupled).astype(BF)

    c = remote(s_one.at[core], s_one.at[core], s_sem.at[0, 0], s_sem.at[1, 0], twin)
    c.start()
    pieces[3].wait_recv()
    local[0].wait()
    c.wait_recv()
    pieces.append(c)
    joined = dot(s_one[0], w_one[0]) + dot(s_one[1], w_one[1])
    s_two[in_quad] = joined[:, 128:].astype(BF)

    arriving = []
    for d in range(1, 4):
        c = remote(
            s_two.at[in_quad],
            s_two.at[in_quad],
            s_sem.at[0, d],
            s_sem.at[1, d],
            quad + lax.rem(in_quad + d, 4),
        )
        c.start()
        arriving.append(c)
    o_first[...] = joined[:, :128]
    outs.append(pltpu.make_async_copy(o_first, first_out, out_sem.at[1]))
    outs[-1].start()
    for c in pieces[4:7]:
        c.wait_recv()
    local[1].wait()
    for c in arriving:
        c.wait_recv()
    pieces += arriving
    joined = dot(s_two[0], w_two[0])
    for i in range(1, 4):
        joined += dot(s_two[i], w_two[i])
    s_three[in_group] = joined[:, 64:].astype(BF)

    arriving = []
    for d in range(1, GROUP):
        c = remote(
            s_three.at[in_group],
            s_three.at[in_group],
            s_sem.at[0, 3 + d],
            s_sem.at[1, 3 + d],
            group + lax.rem(in_group + d, GROUP),
        )
        c.start()
        arriving.append(c)
    o_second[...] = joined[:, :64]
    outs.append(pltpu.make_async_copy(o_second, second_out, out_sem.at[2]))
    outs[-1].start()
    for c in pieces[7:14]:
        c.wait_recv()
    local[2].wait()
    for c in arriving:
        c.wait_recv()
    pieces += arriving
    joined = dot(s_three[0], w_three[0])
    for i in range(1, GROUP):
        joined += dot(s_three[i], w_three[i])
    joined = jnp.where(in_group % 2 == 1, joined[:, 64:], joined[:, :64])
    o_third[...] = joined[:, :32]
    o_top[...] = joined[:, 32:]
    outs.append(pltpu.make_async_copy(o_third, third_out, out_sem.at[3]))
    outs.append(pltpu.make_async_copy(o_top, top_out, out_sem.at[4]))
    for c in outs[3:]:
        c.start()

    handed.wait_send()
    part = pool.at[pl.ds(0, (CHIPS - 1) * 8)]
    pltpu.make_async_copy(part, part, spread_sem.at[0]).wait()
    part = picked.at[pl.ds(0, CHIPS - 1)]
    pltpu.make_async_copy(part, part, gather_sem.at[0]).wait()
    for c in pieces:
        c.wait_send()
    for c in outs:
        c.wait()


def shards(right_sides, block_order, basis, inner, inverse, coupling, one, two, three):
    rows = right_sides.reshape(16, 4, 2, 8, 128).transpose(0, 3, 1, 2, 4)
    leaf = block_order // 8
    order = leaf % 2 * (CHIPS * 8) + leaf // 2 * 8 + block_order % 8
    anywhere = pl.BlockSpec(memory_space=pl.ANY)
    return pl.pallas_call(
        kernel,
        out_shape=(
            jax.ShapeDtypeStruct((128, 768), BF),
            jax.ShapeDtypeStruct((128, 128), F32),
            jax.ShapeDtypeStruct((128, 64), F32),
            jax.ShapeDtypeStruct((128, 32), F32),
            jax.ShapeDtypeStruct((128, 32), F32),
        ),
        in_specs=[pl.BlockSpec(memory_space=pltpu.SMEM)] + [anywhere] * 8,
        out_specs=(anywhere,) * 5,
        scratch_shapes=[
            pltpu.VMEM((16, 8, 4, 2, 128), BF),
            pltpu.VMEM((1024, 2, 128), BF),
            pltpu.VMEM((CHIPS, 8, 2, 128), BF),
            pltpu.VMEM((8, CHIPS, 2, 128), BF),
            pltpu.VMEM((128, 1024), BF),
            pltpu.VMEM((1024, 256), BF),
            pltpu.VMEM((256, 256), BF),
            pltpu.VMEM((768, 768), BF),
            pltpu.VMEM((768, 256), BF),
            pltpu.VMEM((256, 512), BF),
            pltpu.VMEM((128, 512), BF),
            pltpu.VMEM((64, 512), BF),
            pltpu.VMEM((2, 256, 256), BF),
            pltpu.VMEM((4, 128, 128), BF),
            pltpu.VMEM((GROUP, 64, 128), BF),
            pltpu.VMEM((2, 128, 256), BF),
            pltpu.VMEM((4, 128, 128), BF),
            pltpu.VMEM((GROUP, 128, 64), BF),
            pltpu.VMEM((128, 768), BF),
            pltpu.VMEM((128, 128), F32),
            pltpu.VMEM((128, 64), F32),
            pltpu.VMEM((128, 32), F32),
            pltpu.VMEM((128, 32), F32),
            pltpu.SemaphoreType.DMA((8,)),
            pltpu.SemaphoreType.DMA((4,)),
            pltpu.SemaphoreType.DMA((5,)),
            pltpu.SemaphoreType.DMA((2,)),
            pltpu.SemaphoreType.DMA((2,)),
            pltpu.SemaphoreType.DMA((2,)),
            pltpu.SemaphoreType.DMA((2, 4)),
            pltpu.SemaphoreType.DMA((2, 11)),
            pltpu.SemaphoreType.DMA((2, 11)),
        ],
        compiler_params=pltpu.CompilerParams(collective_id=0, has_side_effects=True),
    )(order, rows, basis[0], inner[0], inverse[0], coupling[0], one, two, three)


def solution(mesh):
    return jax.shard_map(
        shards,
        mesh=mesh,
        in_specs=(
            P("rhs", "leaf"),
            P(),
            P("leaf", None, None),
            P("leaf", None, None),
            P("leaf", "rhs", None),
            P("leaf", None, None),
            P("leaf", None),
            P("leaf", None),
            P("leaf", None),
        ),
        out_specs=(P("rhs", "leaf"),) * 5,
        check_vma=False,
    )
```

time: 114 us -> 60.7 us (0.53)
  Pallas kernels: 0 us -> 52.3 us
  waiting for transfers between devices: 46.8 us -> 0 us
  starting transfers between devices: 41 us -> 0 us
  between operations: 14.4 us -> 0.66 us
  matrix products: 3.14 us -> 0 us
    pallas_call x0 -> x1, Pallas kernels: none -> 52.3 us  [shards(): pl.pallas_call(kernel, out_shape=(jax.ShapeDtypeStruct((128, 768), BF), j...]
    all_to_all x2 -> x0, waiting for transfers between devices: 29.7 us -> none  [the longest x1 15.3 us: shards(): lax.all_to_all(returning, 'leaf', split_axis=0, concat_axis=1, tiled=True)]
    all_to_all x2 -> x0, starting transfers between devices: 24 us -> none  [the longest x1 18.4 us: shards(): lax.all_to_all(outgoing, 'leaf', split_axis=0, concat_axis=1, tiled=True)]
    ppermute x6 -> x0, starting transfers between devices: 17 us -> none  [swapped(): return lax.ppermute(block, axis, route)]
    ppermute x6 -> x0, waiting for transfers between devices: 16.4 us -> none  [swapped(): return lax.ppermute(block, axis, route)]
    pallas_call x0 -> x3, local copies, waits for them, and re-layouts: none -> 4.61 us  [shards(): pl.pallas_call(kernel, out_shape=(jax.ShapeDtypeStruct((128, 768), BF), j...]
    gather x1 -> x0, local copies, waits for them, and re-layouts: 3.2 us -> none  [shards(): jnp.take(blocks, block_order, axis=1)]
    dot_general x5 -> x0, matrix products: 2.91 us -> none  [the longest x1 1.6 us: shards(): jnp.dot(leading, lax.all_gather(leaf_inverse, 'rhs', axis=1, tiled=True)[...]
  transfers between devices with their start and end apart: 9 -> 0, of which waited for: 7 -> 0; matrix products, arithmetic and copies ran while one was open for 5% -> 0% of each run, Pallas kernels for 0% -> 0%
where the time goes in v1:
time: 60.7 us; the launch traced here: 60.3 us
  Pallas kernels  52.3 us (86%)
  local copies, waits for them, and re-layouts  6.79 us (11%)
  between operations  0.66 us (1%)
  other arithmetic  0.61 us (1%)
    pallas_call x1, Pallas kernels, shards(): pl.pallas_call(kernel, out_shape=(jax.ShapeDtypeStruct((128, 768), BF), j...  52.3 us
    pallas_call x3, local copies, waits for them, and re-layouts, shards(): pl.pallas_call(kernel, out_shape=(jax.ShapeDtypeStruct((128, 768), BF), j...  4.61 us
    unnamed x8, local copies, waits for them, and re-layouts  2.18 us

profile of v1, /device:TPU:1, one launch (start us, length us, event | category | flops | bytes accessed | tf_op | source)
XLA Modules:
  0.0 60.3 jit_solution(8014509674575817337)
XLA Ops:
  0.6 0.0 copy-start.2
  0.6 0.7 %copy-done.2 = s32[1024]{0:T(1024)S(1)} copy-done((s32[1024]{0:T(1024)S(1)}, s32[1024]{0:T(1024)}, u32[]{:S(2)}) %copy-start.2) | copy-done | bytes 4120
  1.3 0.6 %fusion.2.order = s32[1024]{0:T(1024)} fusion(s32[1024]{0:T(1024)S(1)} %copy-done.2), kind=kLoop, calls=%fused_computation.12 | loop fusion | flops 43008 | bytes 8192 | tf_op jit(solution)/shard_map/add | solution.py:330
  1.9 52.3 %shard_map.128 = (bf16[128,768]{1,0:T(8,128)(2,1)}, f32[128,128]{1,0:T(8,128)}, f32[128,64]{1,0:T(8,128)}, f32[128,32]{1,0:T(8,128)}, f32[128,32]{1,0:T(8,128)}) custom-call(s32[1024]{0:T(1024)} %fusion.2.order, bf16[16,8,4,2,128]{4,3,2,1,0:T(2,128)(2,1)} %bitcast.10, bf16[1024,256]{1,0:T(8,128)(2,1)} %bitcast.7, bf16[256,256]{1,0:T(8,128)(2,1)} %bitcast.11, ...), custom_call_target="tpu_custom_call" | custom-call | tf_op jit(solution)/shard_map/pallas_call | solution.py:332
  54.2 0.0 copy-start
  54.2 1.6 %copy.15 = f32[128,32]{0,1:T(8,128)} copy(f32[128,32]{1,0:T(8,128)} %get-tuple-element.8) | data formatting | bytes 32768 | tf_op jit(solution)/shard_map/pallas_call | solution.py:332
  55.8 1.5 %copy.16 = f32[128,32]{0,1:T(8,128)} copy(f32[128,32]{1,0:T(8,128)} %get-tuple-element.9) | data formatting | bytes 32768 | tf_op jit(solution)/shard_map/pallas_call | solution.py:332
  57.3 1.5 %copy.14 = f32[128,64]{0,1:T(8,128)} copy(f32[128,64]{1,0:T(8,128)} %get-tuple-element.7) | data formatting | bytes 65536 | tf_op jit(solution)/shard_map/pallas_call | solution.py:332
  58.8 0.0 copy-done
  58.8 0.0 copy-start.1
  58.8 0.7 %copy.19 = bf16[128,768]{1,0:T(8,128)(2,1)} copy(bf16[128,768]{1,0:T(8,128)(2,1)S(1)} %copy-done) | data formatting | bytes 393216
  59.5 0.2 copy-done.1
  59.7 0.6 %copy.20 = f32[128,128]{1,0:T(8,128)} copy(f32[128,128]{1,0:T(8,128)S(1)} %copy-done.1) | data formatting | bytes 131072
Async XLA Ops:
  0.6 0.7 %copy-start.2 = (s32[1024]{0:T(1024)S(1)}, s32[1024]{0:T(1024)}, u32[]{:S(2)}) copy-start(s32[1024]{0:T(1024)} %param.10) | copy-start | bytes 12292
  54.2 4.6 %copy-start = (bf16[128,768]{1,0:T(8,128)(2,1)S(1)}, bf16[128,768]{1,0:T(8,128)(2,1)}, u32[]{:S(2)}) copy-start(bf16[128,768]{1,0:T(8,128)(2,1)} %get-tuple-element.15) | copy-start | bytes 589828
  58.8 0.9 %copy-start.1 = (f32[128,128]{1,0:T(8,128)S(1)}, f32[128,128]{1,0:T(8,128)}, u32[]{:S(2)}) copy-start(f32[128,128]{1,0:T(8,128)} %get-tuple-element.16) | copy-start | bytes 196612

commit v2 on v1

--- a/solution.py
+++ b/solution.py
@@ -17,7 +17,7 @@
 
 
 def kernel(
-    order,
+    order_in,
     rows_in,
     basis_in,
     inner_in,
@@ -29,8 +29,8 @@
     leaf_out,
     first_out,
     second_out,
-    third_out,
-    top_out,
+    last_out,
+    order,
     rows,
     pool,
     picked,
@@ -46,17 +46,12 @@
     w_one,
     w_two,
     w_three,
+    w_wide,
     s_one,
     s_two,
     s_three,
-    o_leaf,
-    o_first,
-    o_second,
-    o_third,
-    o_top,
     load_sem,
     own_sem,
-    out_sem,
     spread_sem,
     twin_sem,
     gather_sem,
@@ -73,6 +68,7 @@
     in_quad = me % 4
     quad = me - in_quad
     twin = me + 1 - 2 * core
+    row, column = chip // 8, chip % 8
 
     loads = [
         (rows_in, rows),
@@ -83,6 +79,7 @@
         (basis_in, basis),
         (inner_in, inner),
         (coupling_in, coupling),
+        (order_in, order),
     ]
     loads = [pltpu.make_async_copy(a, b, load_sem.at[i]) for i, (a, b) in enumerate(loads)]
     for load in loads:
@@ -117,26 +114,32 @@
     pl.semaphore_wait(barrier, CHIPS - 1 + GROUP // 2 + PLANES - 1)
 
     loads[0].wait()
-    mine = pl.ds(pl.multiple_of((core * CHIPS + chip) * 8, 8), 8)
-
-    def spread(k, _):
-        other = lax.rem(chip + k, CHIPS)
+    mine = pl.ds(pl.multiple_of(me * 8, 8), 8)
+
+    def step(i):
+        far = (8 - i) // 2
+        return far + (1 - i % 2) * (1 - i // 7) * lax.rem(8 - 2 * far, 8)
+
+    def target(i):
+        return lax.rem(row + step(i // 8), 8) * 8 + lax.rem(column + step(i % 8), 8)
+
+    def spread(i, _):
+        other = target(i)
         remote(
             rows.at[other // 4, :, other % 4],
             pool.at[mine],
-            spread_sem.at[0],
-            spread_sem.at[1],
+            spread_sem.at[8],
+            spread_sem.at[i // 8],
             other * 2 + core,
         ).start()
         return 0
 
-    lax.fori_loop(1, CHIPS, spread, 0)
+    lax.fori_loop(0, CHIPS - 1, spread, 0)
     own = pltpu.make_async_copy(rows.at[chip // 4, :, chip % 4], pool.at[mine], own_sem.at[0])
     own.start()
 
     pieces = []
-    for load in loads[1:5]:
-        load.wait()
+    loads[1].wait()
     for d in range(1, PLANES):
         share = inverse.at[pl.ds(pl.multiple_of(plane * 192, 64), 192)]
         c = remote(
@@ -144,6 +147,52 @@
         )
         c.start()
         pieces.append(c)
+    def hand(i, count):
+        part = pool.at[pl.ds(0, count * 8)]
+        pltpu.make_async_copy(part, part, spread_sem.at[i]).wait()
+        origin = lax.rem(row + 8 - step(i), 8)
+
+        def one_leaf(y, _):
+            block = pool.at[pl.ds(pl.multiple_of(((origin * 8 + y) * 2 + core) * 8, 8), 8)]
+            remote(block, block, twin_sem.at[0], twin_sem.at[1], twin).start()
+            return 0
+
+        lax.fori_loop(0, 8, one_leaf, 0)
+        return 0
+
+    lax.fori_loop(0, 7, lambda i, _: hand(i, 8), 0)
+    own.wait()
+    hand(7, 7)
+    loads[8].wait()
+    half = pool.at[pl.ds(0, CHIPS * 8)]
+    pltpu.make_async_copy(half, half, twin_sem.at[1]).wait()
+
+    def send(other):
+        remote(
+            picked.at[other],
+            placed.at[:, chip],
+            gather_sem.at[0],
+            gather_sem.at[1],
+            other * 2 + core,
+        ).start()
+
+    def gather(i, _):
+        other = target(i)
+        first = (other * 2 + core) * 8
+        for j in range(8):
+            picked[other, j] = pool[order[first + j]]
+
+        @pl.when(i > 0)
+        def _():
+            send(target(i - 1))
+
+        return 0
+
+    lax.fori_loop(0, CHIPS, gather, 0)
+    own = pltpu.make_async_copy(picked.at[chip], placed.at[:, chip], own_sem.at[0])
+    own.start()
+    for load in loads[2:5]:
+        load.wait()
     c = remote(
         one.at[:, pl.ds(pl.multiple_of((1 - core) * 256, 256), 256)],
         w_one.at[core],
@@ -192,40 +241,7 @@
         )
         c.start()
         pieces.append(c)
-
-    own.wait()
-    part = pool.at[pl.ds(0, (CHIPS - 1) * 8)]
-    pltpu.make_async_copy(part, part, spread_sem.at[1]).wait()
-    half = pool.at[pl.ds(pl.multiple_of(core * CHIPS * 8, 8), CHIPS * 8)]
-    handed = remote(half, half, twin_sem.at[0], twin_sem.at[1], twin)
-    handed.start()
-    handed.wait_recv()
-
-    def send(other):
-        remote(
-            picked.at[other],
-            placed.at[:, chip],
-            gather_sem.at[0],
-            gather_sem.at[1],
-            other * 2 + core,
-        ).start()
-
-    def gather(k, _):
-        other = lax.rem(chip + k, CHIPS)
-        first = (other * 2 + core) * 8
-        for j in range(8):
-            picked[other, j] = pool[order[first + j]]
-
-        @pl.when(k > 1)
-        def _():
-            send(lax.rem(chip + k - 1, CHIPS))
-
-        return 0
-
-    lax.fori_loop(1, CHIPS + 1, gather, 0)
-    own = pltpu.make_async_copy(picked.at[chip], placed.at[:, chip], own_sem.at[0])
-    own.start()
-    for load in loads[5:]:
+    for load in loads[5:8]:
         load.wait()
     own.wait()
     part = picked.at[pl.ds(0, CHIPS - 1)]
@@ -242,9 +258,7 @@
     for c in pieces[:3]:
         c.wait_recv()
     eliminated = dot(reflected[:, :768], inverse[...]).astype(BF)
-    o_leaf[...] = eliminated
-    outs = [pltpu.make_async_copy(o_leaf, leaf_out, out_sem.at[0])]
-    outs[0].start()
+    leaf_out[...] = eliminated
     coupled = dot(eliminated, coupling[...])
     s_one[core] = (reflected[:, 768:].astype(F32) - coupled).astype(BF)
 
@@ -268,9 +282,7 @@
         )
         c.start()
         arriving.append(c)
-    o_first[...] = joined[:, :128]
-    outs.append(pltpu.make_async_copy(o_first, first_out, out_sem.at[1]))
-    outs[-1].start()
+    first_out[...] = joined[:, :128]
     for c in pieces[4:7]:
         c.wait_recv()
     local[1].wait()
@@ -280,7 +292,8 @@
     joined = dot(s_two[0], w_two[0])
     for i in range(1, 4):
         joined += dot(s_two[i], w_two[i])
-    s_three[in_group] = joined[:, 64:].astype(BF)
+    low = lax.broadcasted_iota(jnp.int32, (64, 128), 1) < 64
+    s_three[in_group] = jnp.where(low, pltpu.roll(joined[:64], 64, 1), joined[64:]).astype(BF)
 
     arriving = []
     for d in range(1, GROUP):
@@ -293,54 +306,59 @@
         )
         c.start()
         arriving.append(c)
-    o_second[...] = joined[:, :64]
-    outs.append(pltpu.make_async_copy(o_second, second_out, out_sem.at[2]))
-    outs[-1].start()
+    second_out[...] = joined.T[:64]
     for c in pieces[7:14]:
         c.wait_recv()
     local[2].wait()
+    odd = in_group % 2 == 1
+    for i in range(GROUP):
+        w = w_three[i].astype(F32)
+        turned = pltpu.roll(w, 64, 1)
+        w_wide[i, :64] = jnp.where(low, jnp.where(odd, turned, w), 0.0).astype(BF)
+        w_wide[i, 64:] = jnp.where(low, 0.0, jnp.where(odd, w, turned)).astype(BF)
     for c in arriving:
         c.wait_recv()
     pieces += arriving
-    joined = dot(s_three[0], w_three[0])
+    joined = dot(s_three[0], w_wide[0])
     for i in range(1, GROUP):
-        joined += dot(s_three[i], w_three[i])
-    joined = jnp.where(in_group % 2 == 1, joined[:, 64:], joined[:, :64])
-    o_third[...] = joined[:, :32]
-    o_top[...] = joined[:, 32:]
-    outs.append(pltpu.make_async_copy(o_third, third_out, out_sem.at[3]))
-    outs.append(pltpu.make_async_copy(o_top, top_out, out_sem.at[4]))
-    for c in outs[3:]:
-        c.start()
-
-    handed.wait_send()
+        joined += dot(s_three[i], w_wide[i])
+    turned = joined.T
+    last_out[:, :64] = turned[:64]
+    last_out[:, 64:] = turned[64:]
+
+    pltpu.make_async_copy(half, half, twin_sem.at[0]).wait()
     part = pool.at[pl.ds(0, (CHIPS - 1) * 8)]
-    pltpu.make_async_copy(part, part, spread_sem.at[0]).wait()
+    pltpu.make_async_copy(part, part, spread_sem.at[8]).wait()
     part = picked.at[pl.ds(0, CHIPS - 1)]
     pltpu.make_async_copy(part, part, gather_sem.at[0]).wait()
     for c in pieces:
         c.wait_send()
-    for c in outs:
-        c.wait()
+
+
+def finish(leaf_in, first_in, second_in, last_in, leaf, first, second, third, top):
+    leaf[...] = leaf_in[...]
+    first[...] = first_in[...]
+    second[...] = second_in[...]
+    third[...] = last_in[:32]
+    top[...] = last_in[32:]
 
 
 def shards(right_sides, block_order, basis, inner, inverse, coupling, one, two, three):
     rows = right_sides.reshape(16, 4, 2, 8, 128).transpose(0, 3, 1, 2, 4)
-    leaf = block_order // 8
-    order = leaf % 2 * (CHIPS * 8) + leaf // 2 * 8 + block_order % 8
     anywhere = pl.BlockSpec(memory_space=pl.ANY)
-    return pl.pallas_call(
+    vmem = pl.BlockSpec(memory_space=pltpu.VMEM)
+    results = pl.pallas_call(
         kernel,
         out_shape=(
             jax.ShapeDtypeStruct((128, 768), BF),
             jax.ShapeDtypeStruct((128, 128), F32),
-            jax.ShapeDtypeStruct((128, 64), F32),
-            jax.ShapeDtypeStruct((128, 32), F32),
-            jax.ShapeDtypeStruct((128, 32), F32),
-        ),
-        in_specs=[pl.BlockSpec(memory_space=pltpu.SMEM)] + [anywhere] * 8,
-        out_specs=(anywhere,) * 5,
+            jax.ShapeDtypeStruct((64, 128), F32),
+            jax.ShapeDtypeStruct((64, 128), F32),
+        ),
+        in_specs=[anywhere] * 9,
+        out_specs=(vmem,) * 4,
         scratch_shapes=[
+            pltpu.SMEM((1024,), jnp.int32),
             pltpu.VMEM((16, 8, 4, 2, 128), BF),
             pltpu.VMEM((1024, 2, 128), BF),
             pltpu.VMEM((CHIPS, 8, 2, 128), BF),
@@ -356,18 +374,13 @@
             pltpu.VMEM((2, 256, 256), BF),
             pltpu.VMEM((4, 128, 128), BF),
             pltpu.VMEM((GROUP, 64, 128), BF),
+            pltpu.VMEM((GROUP, 128, 128), BF),
             pltpu.VMEM((2, 128, 256), BF),
             pltpu.VMEM((4, 128, 128), BF),
-            pltpu.VMEM((GROUP, 128, 64), BF),
-            pltpu.VMEM((128, 768), BF),
-            pltpu.VMEM((128, 128), F32),
-            pltpu.VMEM((128, 64), F32),
-            pltpu.VMEM((128, 32), F32),
-            pltpu.VMEM((128, 32), F32),
-            pltpu.SemaphoreType.DMA((8,)),
+            pltpu.VMEM((GROUP, 64, 128), BF),
+            pltpu.SemaphoreType.DMA((9,)),
             pltpu.SemaphoreType.DMA((4,)),
-            pltpu.SemaphoreType.DMA((5,)),
-            pltpu.SemaphoreType.DMA((2,)),
+            pltpu.SemaphoreType.DMA((9,)),
             pltpu.SemaphoreType.DMA((2,)),
             pltpu.SemaphoreType.DMA((2,)),
             pltpu.SemaphoreType.DMA((2, 4)),
@@ -375,7 +388,20 @@
             pltpu.SemaphoreType.DMA((2, 11)),
         ],
         compiler_params=pltpu.CompilerParams(collective_id=0, has_side_effects=True),
-    )(order, rows, basis[0], inner[0], inverse[0], coupling[0], one, two, three)
+    )(block_order, rows, basis[0], inner[0], inverse[0], coupling[0], one, two, three)
+    leaf, first, second, third, top = pl.pallas_call(
+        finish,
+        out_shape=(
+            jax.ShapeDtypeStruct((128, 768), BF),
+            jax.ShapeDtypeStruct((128, 128), F32),
+            jax.ShapeDtypeStruct((64, 128), F32),
+            jax.ShapeDtypeStruct((32, 128), F32),
+            jax.ShapeDtypeStruct((32, 128), F32),
+        ),
+        in_specs=[vmem] * 4,
+        out_specs=(vmem,) * 5,
+    )(*results)
+    return leaf, first, second.T, third.T, top.T
 
 
 def solution(mesh):

time: 60.7 us -> 51.5 us (0.85)
  local copies, waits for them, and re-layouts: 6.79 us -> 0 us
  Pallas kernels: 52.3 us -> 50.8 us
  other arithmetic: 0.61 us -> 0 us
    pallas_call x3 -> x0, local copies, waits for them, and re-layouts: 4.61 us -> none  [shards(): pl.pallas_call(kernel, out_shape=(jax.ShapeDtypeStruct((128, 768), BF), j...]
    pallas_call x1, Pallas kernels: 52.3 us -> 49.1 us  [shards(): pl.pallas_call(kernel, out_shape=(jax.ShapeDtypeStruct((128, 768), BF), j...]
    unnamed x8 -> x0, local copies, waits for them, and re-layouts: 2.18 us -> none
    pallas_call x0 -> x1, Pallas kernels: none -> 1.69 us  [shards(): pl.pallas_call(finish, out_shape=(jax.ShapeDtypeStruct((128, 768), BF), j...]
    add x1 -> x0, other arithmetic: 0.61 us -> none  [shards(): order = leaf % 2 * (CHIPS * 8) + leaf // 2 * 8 + block_order % 8]
where the time goes in v2:
time: 51.5 us; the launch traced here: 51.4 us
  Pallas kernels  50.8 us (99%)
  between operations  0.64 us (1%)
    pallas_call x1, Pallas kernels, shards(): pl.pallas_call(kernel, out_shape=(jax.ShapeDtypeStruct((128, 768), BF), j...  49.1 us
    pallas_call x1, Pallas kernels, shards(): pl.pallas_call(finish, out_shape=(jax.ShapeDtypeStruct((128, 768), BF), j...  1.69 us

profile of v2, /device:TPU:1, one launch (start us, length us, event | category | flops | bytes accessed | tf_op | source)
XLA Modules:
  0.0 51.4 jit_solution(11335979682774319470)
XLA Ops:
  0.6 49.1 %shard_map.128 = (bf16[128,768]{1,0:T(8,128)(2,1)}, f32[128,128]{1,0:T(8,128)}, f32[64,128]{1,0:T(8,128)}, f32[64,128]{1,0:T(8,128)}) custom-call(s32[1024]{0:T(1024)} %order_in.1, bf16[16,8,4,2,128]{4,3,2,1,0:T(2,128)(2,1)} %bitcast.13, bf16[1024,256]{1,0:T(8,128)(2,1)} %bitcast.10, bf16[256,256]{1,0:T(8,128)(2,1)} %bitcast.14, bf16[192,768]{1,0:T(8,128)(2,1)} %bitcast.12, ...), custom_call_target="tpu_custom_call" | custom-call | tf_op jit(solution)/shard_map/pallas_call | solution.py:350
  49.7 1.7 %shard_map.129 = (bf16[128,768]{1,0:T(8,128)(2,1)}, f32[128,128]{1,0:T(8,128)}, f32[64,128]{1,0:T(8,128)}, f32[32,128]{1,0:T(8,128)}, f32[32,128]{1,0:T(8,128)}) custom-call(bf16[128,768]{1,0:T(8,128)(2,1)} %get-tuple-element.14.leaf_in, f32[128,128]{1,0:T(8,128)} %get-tuple-element.15.first_in, f32[64,128]{1,0:T(8,128)} %get-tuple-element.16.second_in, ...), custom_call_target="tpu_custom_call" | custom-call | tf_op jit(solution)/shard_map/pallas_call | solution.py:392

commit v3 on v2

--- a/solution.py
+++ b/solution.py
@@ -10,6 +10,7 @@
 CHIPS = 64
 GROUP = 8
 PLANES = 4
+STEPS = (4, 3, 5, 2, 6, 1, 7, 0)
 
 
 def dot(a, b):
@@ -40,6 +41,8 @@
     inner,
     inverse,
     coupling,
+    whole,
+    leading,
     one,
     two,
     three,
@@ -95,6 +98,23 @@
             device_id_type=pl.DeviceIdType.MESH,
         )
 
+    def step(i):
+        far = (8 - i) // 2
+        return far + (1 - i % 2) * (1 - i // 7) * lax.rem(8 - 2 * far, 8)
+
+    columns = [lax.rem(column + STEPS[j], 8) for j in range(8)]
+
+    def each_chip(visit):
+        def one_row(i, _):
+            first = lax.rem(row + step(i), 8) * 8
+            for j in range(8):
+                visit(first + columns[j], i)
+            return 0
+
+        lax.fori_loop(0, 7, one_row, 0)
+        for j in range(7):
+            visit(row * 8 + columns[j], 7)
+
     barrier = pltpu.get_barrier_semaphore()
 
     def greet(target, axis="leaf"):
@@ -102,11 +122,7 @@
             barrier, inc=1, device_id={axis: target}, device_id_type=pl.DeviceIdType.MESH
         )
 
-    def greet_chip(k, _):
-        greet(lax.rem(chip + k, CHIPS) * 2 + core)
-        return 0
-
-    lax.fori_loop(1, CHIPS, greet_chip, 0)
+    each_chip(lambda other, i: greet(other * 2 + core))
     for i in range(GROUP // 2):
         greet(group + 2 * i + 1 - core)
     for d in range(1, PLANES):
@@ -116,25 +132,16 @@
     loads[0].wait()
     mine = pl.ds(pl.multiple_of(me * 8, 8), 8)
 
-    def step(i):
-        far = (8 - i) // 2
-        return far + (1 - i % 2) * (1 - i // 7) * lax.rem(8 - 2 * far, 8)
-
-    def target(i):
-        return lax.rem(row + step(i // 8), 8) * 8 + lax.rem(column + step(i % 8), 8)
-
-    def spread(i, _):
-        other = target(i)
+    def spread(other, i):
         remote(
             rows.at[other // 4, :, other % 4],
             pool.at[mine],
             spread_sem.at[8],
-            spread_sem.at[i // 8],
+            spread_sem.at[i],
             other * 2 + core,
         ).start()
-        return 0
-
-    lax.fori_loop(0, CHIPS - 1, spread, 0)
+
+    each_chip(spread)
     own = pltpu.make_async_copy(rows.at[chip // 4, :, chip % 4], pool.at[mine], own_sem.at[0])
     own.start()
 
@@ -176,19 +183,26 @@
             other * 2 + core,
         ).start()
 
+    def pick(other):
+        first = (other * 2 + core) * 8
+        blocks = [pool[order[first + j]] for j in range(8)]
+        for j in range(8):
+            picked[other, j] = blocks[j]
+
     def gather(i, _):
-        other = target(i)
-        first = (other * 2 + core) * 8
+        first = lax.rem(row + step(i), 8) * 8
         for j in range(8):
-            picked[other, j] = pool[order[first + j]]
-
-        @pl.when(i > 0)
-        def _():
-            send(target(i - 1))
-
+            pick(first + columns[j])
+            if j > 0:
+                send(first + columns[j - 1])
+        send(first + columns[7])
         return 0
 
-    lax.fori_loop(0, CHIPS, gather, 0)
+    lax.fori_loop(0, 7, gather, 0)
+    for j in range(8):
+        pick(row * 8 + columns[j])
+        if j > 0:
+            send(row * 8 + columns[j - 1])
     own = pltpu.make_async_copy(picked.at[chip], placed.at[:, chip], own_sem.at[0])
     own.start()
     for load in loads[2:5]:
@@ -244,26 +258,35 @@
     for load in loads[5:8]:
         load.wait()
     own.wait()
+
+    spread_back = lax.dot_general(
+        inner[...], basis[...], (((1,), (1,)), ((), ())), preferred_element_type=F32
+    )
+    for c in pieces[:3]:
+        c.wait_recv()
+    folded = dot(inverse[...], coupling[...])
+    folded_low = folded.astype(BF)
+    rest = spread_back[:, 768:] - dot(spread_back[:, :768].astype(BF), folded_low)
+    rest = rest.astype(BF)
+    whole[:768] = (folded + dot(basis[:768], rest)).astype(BF)
+    whole[768:] = dot(basis[768:], rest).astype(BF)
+
     part = picked.at[pl.ds(0, CHIPS - 1)]
     pltpu.make_async_copy(part, part, gather_sem.at[1]).wait()
 
     for j in range(8):
         flat[:, j * 128 : (j + 1) * 128] = placed[j].reshape(128, 128)
+    skeleton = flat[:, 768:].astype(F32) - dot(flat[...], whole[...])
+    s_one[core] = skeleton.astype(BF)
+
+    c = remote(s_one.at[core], s_one.at[core], s_sem.at[0, 0], s_sem.at[1, 0], twin)
+    c.start()
     projected = dot(flat[...], basis[...]).astype(BF)
     middle = dot(projected, inner[...]).astype(BF)
     correction = lax.dot_general(
-        middle, basis[...], (((1,), (1,)), ((), ())), preferred_element_type=F32
+        middle, basis[:768], (((1,), (1,)), ((), ())), preferred_element_type=F32
     )
-    reflected = (flat[...].astype(F32) - correction).astype(BF)
-    for c in pieces[:3]:
-        c.wait_recv()
-    eliminated = dot(reflected[:, :768], inverse[...]).astype(BF)
-    leaf_out[...] = eliminated
-    coupled = dot(eliminated, coupling[...])
-    s_one[core] = (reflected[:, 768:].astype(F32) - coupled).astype(BF)
-
-    c = remote(s_one.at[core], s_one.at[core], s_sem.at[0, 0], s_sem.at[1, 0], twin)
-    c.start()
+    leading[...] = (flat[:, :768].astype(F32) - correction).astype(BF)
     pieces[3].wait_recv()
     local[0].wait()
     c.wait_recv()
@@ -283,6 +306,7 @@
         c.start()
         arriving.append(c)
     first_out[...] = joined[:, :128]
+    leaf_out[...] = dot(leading[...], inverse[...]).astype(BF)
     for c in pieces[4:7]:
         c.wait_recv()
     local[1].wait()
@@ -368,6 +392,8 @@
             pltpu.VMEM((256, 256), BF),
             pltpu.VMEM((768, 768), BF),
             pltpu.VMEM((768, 256), BF),
+            pltpu.VMEM((1024, 256), BF),
+            pltpu.VMEM((128, 768), BF),
             pltpu.VMEM((256, 512), BF),
             pltpu.VMEM((128, 512), BF),
             pltpu.VMEM((64, 512), BF),

time: 51.5 us -> 49.2 us (0.955)
  Pallas kernels: 50.8 us -> 48.4 us
    pallas_call x1, Pallas kernels: 49.1 us -> 46.7 us  [shards(): pl.pallas_call(kernel, out_shape=(jax.ShapeDtypeStruct((128, 768), BF), j...]
where the time goes in v3:
time: 49.2 us; the launch traced here: 49 us
  Pallas kernels  48.4 us (98%)
  between operations  0.64 us (1%)
    pallas_call x1, Pallas kernels, shards(): pl.pallas_call(kernel, out_shape=(jax.ShapeDtypeStruct((128, 768), BF), j...  46.7 us
    pallas_call x1, Pallas kernels, shards(): pl.pallas_call(finish, out_shape=(jax.ShapeDtypeStruct((128, 768), BF), j...  1.69 us

profile of v3, /device:TPU:1, one launch (start us, length us, event | category | flops | bytes accessed | tf_op | source)
XLA Modules:
  0.0 49.0 jit_solution(17998944071321525979)
XLA Ops:
  0.6 46.7 %shard_map.128 = (bf16[128,768]{1,0:T(8,128)(2,1)}, f32[128,128]{1,0:T(8,128)}, f32[64,128]{1,0:T(8,128)}, f32[64,128]{1,0:T(8,128)}) custom-call(s32[1024]{0:T(1024)} %order_in.1, bf16[16,8,4,2,128]{4,3,2,1,0:T(2,128)(2,1)} %bitcast.13, bf16[1024,256]{1,0:T(8,128)(2,1)} %bitcast.10, bf16[256,256]{1,0:T(8,128)(2,1)} %bitcast.14, bf16[192,768]{1,0:T(8,128)(2,1)} %bitcast.12, ...), custom_call_target="tpu_custom_call" | custom-call | tf_op jit(solution)/shard_map/pallas_call | solution.py:374
  47.4 1.7 %shard_map.129 = (bf16[128,768]{1,0:T(8,128)(2,1)}, f32[128,128]{1,0:T(8,128)}, f32[64,128]{1,0:T(8,128)}, f32[32,128]{1,0:T(8,128)}, f32[32,128]{1,0:T(8,128)}) custom-call(bf16[128,768]{1,0:T(8,128)(2,1)} %get-tuple-element.14.leaf_in, f32[128,128]{1,0:T(8,128)} %get-tuple-element.15.first_in, f32[64,128]{1,0:T(8,128)} %get-tuple-element.16.second_in, ...), custom_call_target="tpu_custom_call" | custom-call | tf_op jit(solution)/shard_map/pallas_call | solution.py:418

commit v4 on v3

--- a/solution.py
+++ b/solution.py
@@ -73,6 +73,45 @@
     twin = me + 1 - 2 * core
     row, column = chip // 8, chip % 8
 
+    def remote(src, dst, send, recv, target, axis="leaf"):
+        return pltpu.make_async_remote_copy(
+            src_ref=src,
+            dst_ref=dst,
+            send_sem=send,
+            recv_sem=recv,
+            device_id={axis: target},
+            device_id_type=pl.DeviceIdType.MESH,
+        )
+
+    def step(i):
+        far = (8 - i) // 2
+        return far + (1 - i % 2) * (1 - i // 7) * lax.rem(8 - 2 * far, 8)
+
+    columns = [lax.rem(column + STEPS[j], 8) for j in range(8)]
+
+    def each_chip(visit):
+        def one_row(i, _):
+            first = lax.rem(row + step(i), 8) * 8
+            for j in range(8):
+                visit(first + columns[j], i)
+            return 0
+
+        lax.fori_loop(0, 7, one_row, 0)
+        for j in range(7):
+            visit(row * 8 + columns[j], 7)
+
+    barrier = pltpu.get_barrier_semaphore()
+
+    def greet(target, axis="leaf"):
+        pl.semaphore_signal(
+            barrier, inc=1, device_id={axis: target}, device_id_type=pl.DeviceIdType.MESH
+        )
+
+    each_chip(lambda other, i: greet(other * 2 + core))
+    for i in range(GROUP // 2):
+        greet(group + 2 * i + 1 - core)
+    for d in range(1, PLANES):
+        greet(lax.rem(plane + d, PLANES), "rhs")
     loads = [
         (rows_in, rows),
         (inverse_in, inverse.at[pl.ds(pl.multiple_of(plane * 192, 64), 192)]),
@@ -87,46 +126,6 @@
     loads = [pltpu.make_async_copy(a, b, load_sem.at[i]) for i, (a, b) in enumerate(loads)]
     for load in loads:
         load.start()
-
-    def remote(src, dst, send, recv, target, axis="leaf"):
-        return pltpu.make_async_remote_copy(
-            src_ref=src,
-            dst_ref=dst,
-            send_sem=send,
-            recv_sem=recv,
-            device_id={axis: target},
-            device_id_type=pl.DeviceIdType.MESH,
-        )
-
-    def step(i):
-        far = (8 - i) // 2
-        return far + (1 - i % 2) * (1 - i // 7) * lax.rem(8 - 2 * far, 8)
-
-    columns = [lax.rem(column + STEPS[j], 8) for j in range(8)]
-
-    def each_chip(visit):
-        def one_row(i, _):
-            first = lax.rem(row + step(i), 8) * 8
-            for j in range(8):
-                visit(first + columns[j], i)
-            return 0
-
-        lax.fori_loop(0, 7, one_row, 0)
-        for j in range(7):
-            visit(row * 8 + columns[j], 7)
-
-    barrier = pltpu.get_barrier_semaphore()
-
-    def greet(target, axis="leaf"):
-        pl.semaphore_signal(
-            barrier, inc=1, device_id={axis: target}, device_id_type=pl.DeviceIdType.MESH
-        )
-
-    each_chip(lambda other, i: greet(other * 2 + core))
-    for i in range(GROUP // 2):
-        greet(group + 2 * i + 1 - core)
-    for d in range(1, PLANES):
-        greet(lax.rem(plane + d, PLANES), "rhs")
     pl.semaphore_wait(barrier, CHIPS - 1 + GROUP // 2 + PLANES - 1)
 
     loads[0].wait()

time: 49.2 us -> 49.3 us (level)
  no operation moved by 1% of the time
where the time goes in v4:
time: 49.3 us; the launch traced here: 49.2 us
  Pallas kernels  48.5 us (98%)
  between operations  0.64 us (1%)
    pallas_call x1, Pallas kernels, shards(): pl.pallas_call(kernel, out_shape=(jax.ShapeDtypeStruct((128, 768), BF), j...  46.9 us
    pallas_call x1, Pallas kernels, shards(): pl.pallas_call(finish, out_shape=(jax.ShapeDtypeStruct((128, 768), BF), j...  1.69 us

profile of v4, /device:TPU:1, one launch (start us, length us, event | category | flops | bytes accessed | tf_op | source)
XLA Modules:
  0.0 49.2 jit_solution(13983231684863006437)
XLA Ops:
  0.6 46.9 %shard_map.128 = (bf16[128,768]{1,0:T(8,128)(2,1)}, f32[128,128]{1,0:T(8,128)}, f32[64,128]{1,0:T(8,128)}, f32[64,128]{1,0:T(8,128)}) custom-call(s32[1024]{0:T(1024)} %order_in.1, bf16[16,8,4,2,128]{4,3,2,1,0:T(2,128)(2,1)} %bitcast.13, bf16[1024,256]{1,0:T(8,128)(2,1)} %bitcast.10, bf16[256,256]{1,0:T(8,128)(2,1)} %bitcast.14, bf16[192,768]{1,0:T(8,128)(2,1)} %bitcast.12, ...), custom_call_target="tpu_custom_call" | custom-call | tf_op jit(solution)/shard_map/pallas_call | solution.py:373
  47.5 1.7 %shard_map.129 = (bf16[128,768]{1,0:T(8,128)(2,1)}, f32[128,128]{1,0:T(8,128)}, f32[64,128]{1,0:T(8,128)}, f32[32,128]{1,0:T(8,128)}, f32[32,128]{1,0:T(8,128)}) custom-call(bf16[128,768]{1,0:T(8,128)(2,1)} %get-tuple-element.14.leaf_in, f32[128,128]{1,0:T(8,128)} %get-tuple-element.15.first_in, f32[64,128]{1,0:T(8,128)} %get-tuple-element.16.second_in, ...), custom_call_target="tpu_custom_call" | custom-call | tf_op jit(solution)/shard_map/pallas_call | solution.py:417
